TPU v7x, 32 devices: a whole 2x2x4 slice. The times are simulated.
32 devices in a mesh: dp: 2 (over x), rep: 4 (over y, core), ind: 4 (over z).
Axes of the slice: x: 2, y: 2, z: 4, core: 2. Of those that a mesh axis runs over, the one named last changes fastest.
Arguments:
- points: bfloat16 [6144, 64], P(('dp', 'rep')), may hold values from -6 to 6
- targets: float32 [6144], P(('dp', 'rep')), may hold values from -6 to 6
- inducing: float32 [4096, 64], P('ind'), may hold values from -6 to 6
- whitening: bfloat16 [4096, 4096], P('ind'), may hold values from -0.0546875 to 0.0546875
- mean_v: float32 [4096], P('ind'), may hold values from -12 to 12
- covariance: float32 [4096, 4096], P('ind', ('dp', 'rep')), may hold values from -24 to 24
- precision: float32 [4096, 4096], P('ind', ('dp', 'rep')), may hold values from -3 to 3
- natural_one: float32 [4096], P('ind'), may hold values from -6 to 6
- lengthscales: float32 [64], replicated, may hold values from 1.6 to 24
- hypers: float32 [2], replicated, may hold values from 0.5 to 2
Outputs:
- precision_new: float32 [4096, 4096], P('ind', ('dp', 'rep'))
- natural_new: float32 [4096], P('ind')
- expected_fit: float32 [], replicated
All inputs are finite; a program needn't handle non-finite values.
Results may differ from a plain program's by a relative error of at most 0.0076.
Values may be sent and summed in bfloat16 or wider, within the bound.
A program may use at most 128 MiB of HBM per device.

v0:
```python
import jax
import jax.numpy as jnp
from jax import lax
from jax.sharding import PartitionSpec as P


def cross_cov(inducing, points, lengthscales, signal):
    scaled_z = inducing / lengthscales
    scaled_x = points.astype(jnp.float32) / lengthscales
    norm_z = jnp.sum(scaled_z * scaled_z, axis=1)
    norm_x = jnp.sum(scaled_x * scaled_x, axis=1)
    inner = jnp.dot(scaled_z, scaled_x.T, precision=lax.Precision.HIGHEST)
    return (signal * jnp.exp(-0.5 * (norm_z[:, None] + norm_x[None, :] - 2.0 * inner))).astype(
        jnp.bfloat16
    )


def shards(
    points,
    targets,
    inducing,
    whitening,
    mean_v,
    covariance,
    precision,
    natural_one,
    lengthscales,
    hypers,
):
    signal = hypers[0]
    noise_var = hypers[1]
    all_inducing = lax.all_gather(inducing, "ind", axis=0, tiled=True)
    cross = cross_cov(all_inducing, points, lengthscales, signal)
    white = jnp.dot(whitening, cross, preferred_element_type=jnp.float32).astype(jnp.bfloat16)
    white_wide = white.astype(jnp.float32)
    mean_part = jnp.dot(mean_v, white_wide, precision=lax.Precision.HIGHEST)
    square_part = jnp.sum(white_wide * white_wide, axis=0)
    gram_part = lax.dot_general(
        white,
        lax.all_gather(white, "ind", axis=0, tiled=True),
        (((1,), (1,)), ((), ())),
        preferred_element_type=jnp.float32,
    )
    pred_mean, sq_norm = lax.psum((mean_part, square_part), "ind")
    resid = targets - pred_mean
    local_fit = jnp.sum(resid * resid + signal - sq_norm)
    local_proj = jnp.dot(white_wide, targets, precision=lax.Precision.HIGHEST)
    proj, fit_sum = lax.psum((local_proj, local_fit), ("dp", "rep"))
    own_rows = gram_part.shape[0]
    gram = lax.psum_scatter(gram_part, ("dp", "rep"), scatter_dimension=1, tiled=True)
    own_cols = gram.shape[1]
    trace = lax.psum(jnp.sum(covariance * gram), ("dp", "rep", "ind"))
    total = points.shape[0] * lax.axis_size(("dp", "rep"))
    expected_fit = -0.5 * jnp.log(2.0 * jnp.pi * noise_var) - (fit_sum + trace) / (
        2.0 * noise_var * total
    )
    row_ids = lax.axis_index("ind") * own_rows + jnp.arange(own_rows, dtype=jnp.int32)
    col_ids = lax.axis_index(("dp", "rep")) * own_cols + jnp.arange(own_cols, dtype=jnp.int32)
    identity = (row_ids[:, None] == col_ids[None, :]).astype(jnp.float32)
    precision_new = 0.5 * precision + 0.5 * (identity + gram / noise_var)
    natural_new = 0.5 * natural_one + 0.5 * proj / noise_var
    return (precision_new, natural_new, expected_fit)


def solution(mesh):
    return jax.shard_map(
        shards,
        mesh=mesh,
        in_specs=(
            P(("dp", "rep"), None),
            P(("dp", "rep")),
            P("ind", None),
            P("ind", None),
            P("ind"),
            P("ind", ("dp", "rep")),
            P("ind", ("dp", "rep")),
            P("ind"),
            P(),
            P(),
        ),
        out_specs=(P("ind", ("dp", "rep")), P("ind"), P()),
        check_vma=False,
    )
```

profile of v0, /device:TPU:0, one launch (start us, length us, event | category | flops | bytes accessed | tf_op | source)
XLA Modules:
  0.0 361.2 jit_solution(7977664895981380709)
XLA Ops:
  7.2 0.0 copy-start
  7.2 0.0 all-gather.3.cloned.1.call-start
  7.2 0.7 all-gather.3.cloned.1.call-update
  7.9 0.0 all-gather.5.cloned.1.call-start
  8.0 1.3 fusion.4
  9.3 1.0 multiply_reduce_fusion.3
  10.3 30.0 %all-gather.3.cloned.1.call-done = f32[4096,64]{0,1:T(8,128)} async-done(((f32[1024,64]{0,1:T(8,128)}), f32[4096,64]{0,1:T(8,128)}) %all-gather.3.cloned.1.call-update) | async-done | bytes 1048592 | tf_op jit(solution)/shard_map/all_gather | solution.py:32
  40.3 0.0 slice-start
  40.3 1.6 multiply_reduce_fusion.2
  41.9 0.0 slice-start.1
  41.9 14.8 %multiply_convert_fusion = bf16[4096,768]{1,0:T(8,128)(2,1)S(1)} fusion(f32[768]{0:T(1024)S(1)} %multiply_reduce_fusion.3, f32[4096]{0:T(1024)S(1)} %multiply_reduce_fusion.2, f32[]{:T(128)} %bitcast, f32[4096,64]{0,1:T(8,128)} %all-gather.3.cloned.1.call-done, f32[64]{0:T(128)} %param.18, bf16[768,64]{0,1:T(8,128)(2,1)} %param.10), kind=kOutput, calls=%fused_computation | convolution fusion | flops 2435153920 | bytes 7458052 | tf_op jit(solution)/shard_map/dot_general | solution.py:12
  56.7 0.0 slice-done
  56.7 0.0 slice-done.1
  56.7 7.9 %multiply_reduce_fusion = (f32[768]{0:T(1024)S(1)}, bf16[768,1024]{1,0:T(8,128)(2,1)}) fusion(bf16[4096,768]{1,0:T(8,128)(2,1)S(1)} %multiply_convert_fusion, bf16[1024,4096]{1,0:T(8,128)(2,1)S(1)} %bitcast.20), kind=kOutput, calls=%fused_computation.1 | convolution fusion | flops 6445595648 | bytes 16256000 | tf_op jit(solution)/shard_map/dot_general | solution.py:34
  64.6 0.0 all-gather.5.cloned.1.call-update
  64.6 0.2 reduce-scatter.2.cloned.1.call-start
  64.8 114.6 %all-gather.5.cloned.1.call-done = bf16[4096,768]{0,1:T(8,128)(2,1)} async-done(((bf16[1024,768]{0,1:T(8,128)(2,1)}), bf16[4096,768]{0,1:T(8,128)(2,1)}) %all-gather.5.cloned.1.call-update) | async-done | bytes 6291472 | tf_op jit(solution)/shard_map/all_gather | solution.py:40
  179.5 12.5 %fusion.5 = f32[1024,4096]{1,0:T(8,128)} fusion(bf16[768,1024]{1,0:T(8,128)(2,1)} %get-tuple-element.12, bf16[4096,768]{0,1:T(8,128)(2,1)} %all-gather.5.cloned.1.call-done), kind=kOutput, calls=%fused_computation.19 | convolution fusion | flops 6442450944 | bytes 24641536 | tf_op jit(solution)/shard_map/dot_general | solution.py:38
  192.0 0.0 copy-start.2
  192.0 0.0 copy-start.1
  192.0 0.0 reduce-scatter.2.cloned.1.call-update
  192.0 0.0 copy-start.3
  192.1 0.6 copy-done.2
  194.1 0.0 copy-done
  194.1 0.0 copy-done.1
  194.1 1.3 convolution_reduce_fusion
  195.4 8.8 %all-reduce.1 = (f32[768]{0:T(1024)S(1)}, f32[768]{0:T(1024)S(1)}) all-reduce(f32[768]{0:T(1024)S(1)} %get-tuple-element.11, f32[768]{0:T(1024)S(1)} %convolution_reduce_fusion), channel_id=1, replica_groups=mesh['dp'=2,'rep'=4,'ind'=4] {'ind'}, use_global_device_ids=true, to_apply=%region_6.0 | all-reduce | flops 1536 | bytes 12288 | tf_op jit(solution)/shard_map/psum | solution.py:44
  204.2 1.3 subtract_reduce_fusion
  205.5 0.7 fusion.2
  206.2 12.9 %all-reduce = (f32[1024]{0:T(1024)S(1)}, f32[]{:T(128)}) all-reduce(f32[1024]{0:T(1024)S(1)} %bitcast.18, f32[]{:T(128)} %subtract_reduce_fusion), channel_id=1, replica_groups=mesh['dp'=2,'rep'=4,'ind'=4] {'dp','rep'}, use_global_device_ids=true, to_apply=%region_3.0 | all-reduce | flops 1025 | bytes 8200 | tf_op jit(solution)/shard_map/psum | solution.py:48
  219.2 0.0 copy-done.3
  219.2 1.2 divide_add_fusion
  220.4 86.0 %reduce-scatter.2.cloned.1.call-done = f32[1024,512]{1,0:T(8,128)} async-done(((f32[1024,4096]{1,0:T(8,128)}), f32[1024,512]{1,0:T(8,128)}) %reduce-scatter.2.cloned.1.call-update) | async-done | bytes 2097168 | tf_op jit(solution)/shard_map/reduce_scatter | solution.py:50
  306.4 6.4 %multiply_reduce_fusion.1 = (f32[]{:T(128)}, f32[1024,512]{1,0:T(8,128)}) fusion(f32[1024,512]{1,0:T(8,128)} %param.15, f32[1024,512]{1,0:T(8,128)} %reduce-scatter.2.cloned.1.call-done, f32[1024,512]{1,0:T(8,128)} %param.16, f32[]{:T(128)} %bitcast.2, s32[512]{0:T(512)S(1)} %iota_add_fusion.1, s32[1024]{0:T(1024)S(1)} %iota_add_fusion), kind=kLoop, calls=%fused_computation.2 | loop fusion | flops 4194303 | bytes 8394760 | tf_op jit(solution)/shard_map/reduce_sum | solution.py:52
  312.8 39.5 %psum.39 = f32[]{:T(128)} all-reduce(f32[]{:T(128)} %get-tuple-element.7), channel_id=1, replica_groups=mesh['dp'=2,'rep'=4,'ind'=4] {'dp','rep','ind'}, use_global_device_ids=true, to_apply=%region_10.0 | all-reduce | flops 1 | bytes 8 | tf_op jit(solution)/shard_map/psum | solution.py:52
  (4 shorter events, 0.0 us)
Async XLA Ops:
  7.2 186.9 %copy-start = (f32[1024]{0:T(1024)S(1)}, f32[1024]{0:T(1024)}, u32[]{:S(2)}) copy-start(f32[1024]{0:T(1024)} %param.14) | copy-start | bytes 12292
  7.2 33.1 %all-gather.3.cloned.1.call-start = ((), (), s32[]{:S(2)}) async-start(), calls=%async_computation.1 | async-start | bytes 1310720 | tf_op jit(solution)/shard_map/all_gather | solution.py:32
  7.9 171.6 %all-gather.5.cloned.1.call-start = ((), (), s32[]{:S(2)}) async-start(), calls=%async_computation.2 | async-start | bytes 7864320 | tf_op jit(solution)/shard_map/all_gather | solution.py:40
  40.3 16.4 %slice-start = ((s8[8388608]{0:T(1024)(128)(4,1)}), s8[4194304]{0:T(1024)(128)(4,1)S(1)}, s32[]{:S(2)}) async-start(s8[8388608]{0:T(1024)(128)(4,1)} %bitcast.19), calls=%async_computation.4 | async-start | bytes 8388608
  41.9 14.8 %slice-start.1 = ((s8[8388608]{0:T(1024)(128)(4,1)}), s8[4194304]{0:T(1024)(128)(4,1)S(1)}, s32[]{:S(2)}) async-start(s8[8388608]{0:T(1024)(128)(4,1)} %bitcast.19), calls=%async_computation.5 | async-start | bytes 8388608
  64.6 241.8 %reduce-scatter.2.cloned.1.call-start = ((), (), s32[]{:S(2)}) async-start(), calls=%async_computation.3 | async-start | bytes 18874368 | tf_op jit(solution)/shard_map/reduce_scatter | solution.py:50
  192.0 0.7 copy-start.2
  192.0 2.1 copy-start.1
  192.0 27.1 %copy-start.3 = (f32[1024]{0:T(1024)S(1)}, f32[1024]{0:T(1024)}, u32[]{:S(2)}) copy-start(f32[1024]{0:T(1024)} %param.17) | copy-start | bytes 12292
Sparse Core Ops, SparseCore 0:
  9.6 30.6 all-gather.2
  64.7 114.6 all-gather.4
  192.2 114.2 reduce-scatter.1
where the time goes:
time: 362 us; the launch traced here: 361 us
  waiting for transfers between devices  231 us (64%)
  blocking collectives  61.2 us (17%)
  matrix products  37.2 us (10%)
  between operations  17.6 us (5%)
  other arithmetic  11.5 us (3%)
    all_gather x1, waiting for transfers between devices, shards(): lax.all_gather(white, 'ind', axis=0, tiled=True)  115 us
    reduce_scatter x1, waiting for transfers between devices, shards(): lax.psum_scatter(gram_part, ('dp', 'rep'), scatter_dimension=1, tiled=True)  86 us
    psum x1, blocking collectives, shards(): trace = lax.psum(jnp.sum(covariance * gram), ('dp', 'rep', 'ind'))  39.5 us
    all_gather x1, waiting for transfers between devices, shards(): all_inducing = lax.all_gather(inducing, 'ind', axis=0, tiled=True)  30 us
    dot_general x1, matrix products, cross_cov(): inner = jnp.dot(scaled_z, scaled_x.T, precision=lax.Precision.HIGHEST)  14.8 us
    psum x1, blocking collectives, shards(): proj, fit_sum = lax.psum((local_proj, local_fit), ('dp', 'rep'))  12.9 us
    dot_general x1, matrix products, shards(): lax.dot_general(white, lax.all_gather(white, 'ind', axis=0, tiled=True),...  12.5 us
    psum x1, blocking collectives, shards(): pred_mean, sq_norm = lax.psum((mean_part, square_part), 'ind')  8.8 us
  transfers between devices with their start and end apart: 3, of which 3 were waited for; matrix products, arithmetic and copies ran while one was open for 2% of the time, Pallas kernels for 0%

commit v1 on v0

v1 whole, which is shorter than its diff:
```python
import math

import jax
import jax.numpy as jnp
from jax import lax
from jax.sharding import Mesh, PartitionSpec as P

LOG2E = math.log2(math.e)
CHUNKS = 2
CROSS_BYTES = 2**25
PLANE = ("dp", "row")


def split3(value):
    high = lax.reduce_precision(value, 8, 7)
    rest = value - high
    mid = lax.reduce_precision(rest, 8, 7)
    low = rest - mid
    return [part.astype(jnp.bfloat16) for part in (high, mid, low)]


def dot_t(left, right):
    return lax.dot_general(
        left, right, (((1,), (1,)), ((), ())), preferred_element_type=jnp.float32
    )


def sum_over(value, axes):
    for axis in axes:
        size, turn = lax.axis_size(axis), 1
        while turn < size:
            value = value + lax.ppermute(value, axis, [(q, q ^ turn) for q in range(size)])
            turn *= 2
    return value


def shards(
    points,
    targets,
    inducing,
    whitening,
    mean_v,
    covariance,
    precision,
    natural_one,
    lengthscales,
    hypers,
):
    signal = hypers[0]
    noise_var = hypers[1]
    own_rows, width = whitening.shape
    own_cols = covariance.shape[1]
    planes = lax.axis_size("ind")
    chips = lax.axis_size(PLANE)
    side = lax.axis_index("core")
    chip = lax.axis_index(PLANE)
    groups = chips // planes
    total = points.shape[0] * chips * 2
    features = points.shape[1]

    strip = own_cols // (CHUNKS * chips)
    mine = lax.dynamic_index_in_dim(
        whitening.reshape(groups, 2, CHUNKS, chips, strip, width), side, 1, keepdims=False
    )
    mine = lax.dynamic_index_in_dim(mine, chip, 2, keepdims=False)
    gathered = [
        lax.all_gather(mine[:, at], "ind", axis=0, tiled=True) for at in range(CHUNKS)
    ]

    points_t = jnp.concatenate([points] + [part[:, None] for part in split3(targets)], axis=1)
    half = lax.all_gather(points_t, PLANE, axis=0, tiled=True)
    half_points, half_targets = half[:, :features], half[:, features:]
    feats = jnp.concatenate([inducing, mean_v[:, None]], axis=1).T
    seat = own_rows // (2 * chips)
    feats = lax.dynamic_slice_in_dim(feats, (chip * 2 + side) * seat, seat, 1)
    feats = lax.all_gather(feats, "ind", axis=1)
    middle = feats.shape[0] // 2
    feats = jnp.concatenate(
        [
            lax.all_gather(part, PLANE + ("core",), axis=2).reshape(part.shape[0], -1)
            for part in (feats[:middle], feats[middle:])
        ],
        axis=0,
    )
    all_inducing = feats[:features]
    all_mean = feats[features]

    scale_in = lengthscales[:, None]
    scaled_z = all_inducing / scale_in
    norm_z = jnp.log2(signal) - (0.5 * LOG2E) * jnp.sum(scaled_z * scaled_z, axis=0)
    weights = split3((scaled_z / scale_in) * LOG2E)
    left = jnp.concatenate(
        weights
        + [part[None, :] for part in split3(norm_z)]
        + [jnp.ones((3, all_inducing.shape[1]), jnp.bfloat16)],
        axis=0,
    )
    scaled_x = half_points.astype(jnp.float32) / lengthscales
    norm_x = (-0.5 * LOG2E) * jnp.sum(scaled_x * scaled_x, axis=1)
    right = jnp.concatenate(
        [half_points] * 3
        + [jnp.ones((half_points.shape[0], 3), jnp.bfloat16)]
        + [part[:, None] for part in split3(norm_x)],
        axis=1,
    )

    def cross_of(block):
        args = lax.dot_general(
            left, block, (((0,), (1,)), ((), ())), preferred_element_type=jnp.float32
        )
        return jnp.exp2(args).astype(jnp.bfloat16)

    def white_of(weight, cross):
        white = jnp.dot(weight, cross, preferred_element_type=jnp.float32).astype(jnp.bfloat16)
        return lax.optimization_barrier(white)

    swap = [(0, 1), (1, 0)]

    def send(piece):
        gots = []
        for turn in range(1, chips):
            sent = lax.dynamic_index_in_dim(piece, chip ^ turn, 0)
            gots.append(lax.ppermute(sent, PLANE, [(q, q ^ turn) for q in range(chips)]))
        return gots

    def assemble(piece, gots):
        strips = jnp.zeros(piece.shape, piece.dtype)
        own = lax.dynamic_index_in_dim(piece, chip, 0)
        strips = lax.dynamic_update_slice_in_dim(strips, own, chip, 0)
        for turn, got in enumerate(gots, 1):
            strips = lax.dynamic_update_slice_in_dim(strips, got, chip ^ turn, 0)
        return strips.reshape(chips * strip, width)

    def both_of(strips):
        return jnp.concatenate([strips, lax.ppermute(strips, "core", swap)], axis=0)

    def block_terms(block, block_targets, ready=None):
        cross = cross_of(block)
        white = white_of(whitening, cross)
        if ready is None:
            gots, white = lax.optimization_barrier((send(gathered[0]), white))
            grams = []
            for at in range(CHUNKS):
                strips = both_of(assemble(gathered[at], gots))
                if at + 1 < CHUNKS:
                    strips, piece = lax.optimization_barrier((strips, gathered[at + 1]))
                    right_white = white_of(strips, cross)
                    gots, right_white = lax.optimization_barrier((send(piece), right_white))
                    gram = dot_t(white, right_white)
                else:
                    gram = dot_t(white, white_of(strips, cross))
                grams.append(gram)
        else:
            grams = [dot_t(white, white_of(weight, cross)) for weight in ready]
        proj = jnp.sum(
            jnp.dot(white, block_targets, preferred_element_type=jnp.float32), axis=1
        )
        size = chips * strip
        return [part[:, :size] for part in grams], [part[:, size:] for part in grams], proj

    count = half_points.shape[0]
    blocks = 1
    while 2 * width * (count // blocks) > CROSS_BYTES:
        blocks *= 2
    if blocks == 1:
        own_gram, other_gram, proj_part = block_terms(right, half_targets)
    else:
        ready = [both_of(assemble(piece, send(piece))) for piece in gathered]

        def step(carry, pieces):
            return jax.tree.map(jnp.add, carry, block_terms(*pieces, ready)), None

        pieces = (
            right.reshape(blocks, count // blocks, -1),
            half_targets.reshape(blocks, count // blocks, -1),
        )
        start = jax.tree.map(
            lambda leaf: jnp.zeros(leaf.shape, leaf.dtype),
            jax.eval_shape(block_terms, pieces[0][0], pieces[1][0], ready),
        )
        (own_gram, other_gram, proj_part), unused = lax.scan(step, start, pieces)

    got = [lax.ppermute(part, "core", swap) for part in other_gram]
    gram = jnp.concatenate([a + b for a, b in zip(own_gram, got)], axis=1)
    proj = proj_part + lax.ppermute(proj_part, "core", swap)

    first_row = lax.axis_index("ind") * own_rows
    col = chip * 2 + side
    row_ids = first_row + jnp.arange(own_rows, dtype=jnp.int32)
    col_ids = col * own_cols + jnp.arange(own_cols, dtype=jnp.int32)
    identity = (row_ids[:, None] == col_ids[None, :]).astype(jnp.float32)
    col_mean = lax.dynamic_slice_in_dim(all_mean, col * own_cols, own_cols, 0)
    quad = jnp.sum((covariance + mean_v[:, None] * col_mean[None, :] - identity) * gram)
    once = jnp.where(col == 0, -2.0 * jnp.sum(mean_v * proj), 0.0)
    squares = jnp.where(lax.axis_index("ind") == 0, jnp.sum(targets * targets), 0.0)
    local = (quad + once + squares).reshape(1)
    fit_all = sum_over(local, ("core",) + PLANE + ("ind",))[0] + signal * total
    expected_fit = -0.5 * jnp.log(2.0 * jnp.pi * noise_var) - fit_all / (2.0 * noise_var * total)
    precision_new = 0.5 * precision + 0.5 * (identity + gram / noise_var)
    natural_new = 0.5 * natural_one + 0.5 * proj / noise_var
    return (precision_new, natural_new, expected_fit)


def solution(mesh):
    sizes = mesh.shape
    names = ("dp", "row", "core", "ind")
    pairs = Mesh(
        mesh.devices.reshape(sizes["dp"], sizes["rep"] // 2, 2, sizes["ind"]), names
    )
    cols = ("dp", "row", "core")
    return jax.shard_map(
        shards,
        mesh=pairs,
        in_specs=(
            P(cols, None),
            P(cols),
            P("ind", None),
            P("ind", None),
            P("ind"),
            P("ind", cols),
            P("ind", cols),
            P("ind"),
            P(),
            P(),
        ),
        out_specs=(P("ind", cols), P("ind"), P()),
        check_vma=False,
    )
```

time: 362 us -> 246 us (0.68)
  waiting for transfers between devices: 231 us -> 10.3 us
  matrix products: 37.2 us -> 99.7 us
  local copies, waits for them, and re-layouts: 1.99 us -> 34.5 us
  starting transfers between devices: 0.3 us -> 19.6 us
  blocking collectives: 61.2 us -> 45.4 us
  between operations: 17.6 us -> 23.8 us
    all_gather x2, waiting for transfers between devices: 145 us -> 0.02 us  [shards(): lax.all_gather(mine[:, at], 'ind', axis=0, tiled=True)]
    reduce_scatter x1 -> x0, waiting for transfers between devices: 86 us -> none  [shards(): lax.psum_scatter(gram_part, ('dp', 'rep'), scatter_dimension=1, tiled=True)]
    dot_general x5 -> x7, matrix products: 37.2 us -> 99.7 us  [the longest x3 73.4 us: white_of(): jnp.dot(weight, cross, preferred_element_type=jnp.float32)]
    psum x3 -> x0, blocking collectives: 61.2 us -> none  [the longest x1 39.5 us: shards(): trace = lax.psum(jnp.sum(covariance * gram), ('dp', 'rep', 'ind'))]
    all_gather x0 -> x4, blocking collectives: none -> 45.4 us  [the longest x2 19 us: shards(): lax.all_gather(part, PLANE + ('core',), axis=2).reshape(part.shape[0], -1)]
    ppermute x0 -> x16, starting transfers between devices: none -> 19.6 us  [the longest x5 11.6 us: sum_over(): lax.ppermute(value, axis, [(q, q ^ turn) for q in range(size)])]
    unnamed x13 -> x42, local copies, waits for them, and re-layouts: 0.68 us -> 11.3 us
    concatenate x0 -> x2, local copies, waits for them, and re-layouts: none -> 9.79 us  [the longest x1 4.97 us: shards(): jnp.concatenate(weights + [part[None, :] for part in split3(norm_z)] + [j...]
  transfers between devices with their start and end apart: 3 -> 18, of which waited for: 3 -> 6; matrix products, arithmetic and copies ran while one was open for 2% -> 53% of each run, Pallas kernels for 0% -> 0%
where the time goes in v1:
time: 246 us; the launch traced here: 245 us
  matrix products  99.7 us (41%)
  blocking collectives  45.4 us (18%)
  local copies, waits for them, and re-layouts  34.5 us (14%)
  between operations  23.8 us (10%)
  starting transfers between devices  19.6 us (8%)
  other arithmetic  11.9 us (5%)
  waiting for transfers between devices  10.3 us (4%)
    dot_general x3, matrix products, white_of(): jnp.dot(weight, cross, preferred_element_type=jnp.float32)  73.4 us
    all_gather x2, blocking collectives, shards(): lax.all_gather(part, PLANE + ('core',), axis=2).reshape(part.shape[0], -1)  19 us
    all_gather x1, blocking collectives, shards(): feats = lax.all_gather(feats, 'ind', axis=1)  15.7 us
    dot_general x1, matrix products, cross_of(): lax.dot_general(left, block, (((0,), (1,)), ((), ())), preferred_element_...  13.5 us
    dot_general x2, matrix products, dot_t(): lax.dot_general(left, right, (((1,), (1,)), ((), ())), preferred_element_...  11.9 us
    ppermute x5, starting transfers between devices, sum_over(): lax.ppermute(value, axis, [(q, q ^ turn) for q in range(size)])  11.6 us
    unnamed x42, local copies, waits for them, and re-layouts  11.3 us
    all_gather x1, blocking collectives, shards(): half = lax.all_gather(points_t, PLANE, axis=0, tiled=True)  10.8 us
  transfers between devices with their start and end apart: 18, of which 6 were waited for; matrix products, arithmetic and copies ran while one was open for 53% of the time, Pallas kernels for 0%

profile of v1, /device:TPU:0, one launch (start us, length us, event | category | flops | bytes accessed | tf_op | source)
XLA Modules:
  0.0 245.4 jit_solution(2015794139248130180)
XLA Ops:
  7.2 1.3 dynamic-slice_bitcast_fusion
  8.6 1.0 fusion.15
  10.4 15.7 %all-gather.1 = f32[65,512]{1,0:T(8,128)S(1)} all-gather(f32[65,128]{1,0:T(8,128)S(1)} %fusion.9), channel_id=3, replica_groups=mesh['dp'=2,'row'=2,'core'=2,'ind'=4] {'ind'}, dimensions={1}, use_global_device_ids=true | all-gather | bytes 166400 | tf_op jit(solution)/shard_map/all_gather | solution.py:76
  26.9 10.8 %all_gather.34 = bf16[3072,67]{0,1:T(8,128)(2,1)S(1)} all-gather(bf16[768,67]{0,1:T(8,128)(2,1)S(1)} %pad_maximum_fusion.3), channel_id=1, replica_groups=mesh['dp'=2,'row'=2,'core'=2,'ind'=4] {'dp','row'}, dimensions={0}, use_global_device_ids=true | all-gather | bytes 514560 | tf_op jit(solution)/shard_map/all_gather | solution.py:71
  37.9 9.3 %all-gather.3 = f32[33,4,1024]{2,1,0:T(4,128)S(1)} all-gather(f32[33,4,128]{2,1,0:T(4,128)S(1)} %reshape.143), channel_id=5, replica_groups=mesh['dp'=2,'row'=2,'core'=2,'ind'=4] {'dp','row','core'}, dimensions={2}, use_global_device_ids=true | all-gather | bytes 608256 | tf_op jit(solution)/shard_map/all_gather | solution.py:80
  47.8 9.7 %all-gather.2 = f32[32,4,1024]{2,1,0:T(4,128)S(1)} all-gather(f32[32,4,128]{2,1,0:T(4,128)S(1)} %reshape.141), channel_id=4, replica_groups=mesh['dp'=2,'row'=2,'core'=2,'ind'=4] {'dp','row','core'}, dimensions={2}, use_global_device_ids=true | all-gather | bytes 589824 | tf_op jit(solution)/shard_map/all_gather | solution.py:80
  60.0 4.8 %concatenate.28 = bf16[3072,198]{0,1:T(8,128)(2,1)} concatenate(bf16[3072,64]{0,1:T(8,128)(2,1)S(1)} %slice-done.2, bf16[3072,64]{0,1:T(8,128)(2,1)S(1)} %slice-done.2, bf16[3072,64]{0,1:T(8,128)(2,1)S(1)} %slice-done.2, bf16[3072,3]{0,1:T(4,128)(2,1)S(1)} %broadcast_in_dim.17, bf16[3072,1]{0,1:T(2,128)(2,1)S(1)} %get-tuple-element.49, bf16[3072,1]{0,1:T(2,128)(2,1)S(1)} %get-tuple-element.48, ...), dimensions={1} | concatenate | bytes 2433024 | tf_op jit(solution)/shard_map/concatenate | solution.py:100
  64.9 5.0 %concatenate.26 = bf16[198,4096]{1,0:T(8,128)(2,1)} concatenate(bf16[64,4096]{1,0:T(8,128)(2,1)S(1)} %get-tuple-element.43, bf16[64,4096]{1,0:T(8,128)(2,1)S(1)} %get-tuple-element.42, bf16[64,4096]{1,0:T(8,128)(2,1)S(1)} %get-tuple-element.29, bf16[1,4096]{1,0:T(2,128)(2,1)S(1)} %get-tuple-element.46, bf16[1,4096]{1,0:T(2,128)(2,1)S(1)} %get-tuple-element.45, ...), dimensions={0} | concatenate | bytes 3244032 | tf_op jit(solution)/shard_map/concatenate | solution.py:92
  69.9 13.5 %exponential_convert_fusion = bf16[4096,3072]{1,0:T(8,128)(2,1)} fusion(bf16[198,4096]{1,0:T(8,128)(2,1)} %concatenate.26, bf16[3072,198]{0,1:T(8,128)(2,1)} %concatenate.28), kind=kOutput, calls=%fused_computation | convolution fusion | flops 5007998976 | bytes 28004352 | tf_op jit(solution)/shard_map/dot_general | solution.py:108
  83.3 1.5 dynamic-slice_bitcast_fusion.1
  84.8 0.9 collective-permute-start
  85.7 1.2 collective-permute-start.1
  86.9 1.4 collective-permute-start.2
  88.4 33.3 %convert_bitcast_fusion = bf16[1024,3072]{0,1:T(8,128)(2,1)} fusion(bf16[4096,3072]{1,0:T(8,128)(2,1)} %exponential_convert_fusion, bf16[1024,4096]{1,0:T(8,128)(2,1)} %param.13), kind=kOutput, calls=%fused_computation.1 | convolution fusion | flops 25772949504 | bytes 39845888 | tf_op jit(solution)/shard_map/dot_general | solution.py:114
  121.9 1.1 bitcast_dynamic-update-slice_fusion.1
  123.3 1.6 broadcast.73.clone
  125.6 0.8 bitcast_dynamic-update-slice_fusion
  126.5 1.1 collective-permute-done.3
  127.5 2.0 pad_maximum_fusion
  129.7 0.9 collective-permute-start.4
  130.5 1.2 collective-permute-start.5
  131.8 1.5 collective-permute-start.6
  133.2 19.2 %convolution_convert_fusion.1 = bf16[512,3072]{1,0:T(8,128)(2,1)} fusion(bf16[512,4096]{1,0:T(8,128)(2,1)S(1)} %pad_maximum_fusion, bf16[4096,3072]{1,0:T(8,128)(2,1)} %exponential_convert_fusion), kind=kOutput, calls=%fused_computation.3 | convolution fusion | flops 12886474752 | bytes 32505856 | tf_op jit(solution)/shard_map/dot_general | solution.py:114
  152.4 3.7 %collective-permute-done.6 = bf16[1,64,4096]{2,1,0:T(8,128)(2,1)S(1)} collective-permute-done((bf16[1,64,4096]{2,1,0:T(8,128)(2,1)S(1)}, bf16[1,64,4096]{2,1,0:T(8,128)(2,1)S(1)}, u32[]{:S(2)}, u32[]{:S(2)}) %collective-permute-start.6) | collective-permute-done | bytes 524320 | tf_op jit(solution)/shard_map/ppermute | solution.py:123
  156.1 0.8 constant_dynamic-update-slice_fusion.2
  157.8 0.8 constant_dynamic-update-slice_fusion
  158.6 6.5 %fusion.17 = f32[1024,512]{0,1:T(8,128)S(1)} fusion(bf16[512,3072]{1,0:T(8,128)(2,1)} %convolution_convert_fusion.1, bf16[1024,3072]{0,1:T(8,128)(2,1)} %convert_bitcast_fusion), kind=kOutput, calls=%fused_computation.75 | convolution fusion | flops 3221225472 | bytes 11534336 | tf_op jit(solution)/shard_map/dot_general | solution.py:23
  165.1 1.3 copy-done.3
  166.4 1.1 slice.66
  167.9 20.9 %convolution_convert_fusion = bf16[512,3072]{1,0:T(8,128)(2,1)} fusion(bf16[4096,3072]{1,0:T(8,128)(2,1)} %exponential_convert_fusion, bf16[256,4096]{1,0:T(8,128)(2,1)} %collective-permute-done.8, bf16[256,4096]{1,0:T(8,128)(2,1)} %bitcast.15), kind=kOutput, calls=%fused_computation.2 | convolution fusion | flops 12894863360 | bytes 32505856 | tf_op jit(solution)/shard_map/dot_general | solution.py:114
  188.9 5.4 %fusion.18 = f32[1024,512]{0,1:T(8,128)S(1)} fusion(bf16[512,3072]{1,0:T(8,128)(2,1)} %convolution_convert_fusion, bf16[1024,3072]{0,1:T(8,128)(2,1)S(1)} %bitcast.54), kind=kOutput, calls=%fused_computation.76 | convolution fusion | flops 3221225472 | bytes 11534336 | tf_op jit(solution)/shard_map/dot_general | solution.py:23
  194.3 1.1 slice.68
  195.6 0.9 convolution_reduce_fusion
  196.9 1.9 copy.17
  198.9 2.9 %copy.18 = f32[1024,512]{0,1:T(8,128)} copy(f32[1024,512]{1,0:T(8,128)} %param.15) | data formatting | bytes 4194304 | tf_op args[5]
  204.5 1.9 multiply_reduce_fusion.3
  207.1 1.5 slice_add_fusion.1
  209.0 1.5 slice_add_fusion
  210.6 3.4 %fusion.6 = (f32[]{:T(128)}, f32[1024,512]{0,1:T(8,128)}) fusion(f32[1024,512]{0,1:T(8,128)S(1)} %copy-done, f32[1024,256]{0,1:T(8,128)S(1)} %slice_add_fusion, f32[1024,256]{0,1:T(8,128)S(1)} %slice_add_fusion.1, f32[512]{0:T(512)S(1)} %dynamic_slice.47, f32[1024]{0:T(1024)S(1)} %copy-done.10, s32[1024]{0:T(1024)S(1)} %iota_add_fusion, ...), kind=kLoop, calls=%fused_computation.13 | loop fusion | flops 6291455 | bytes 8400904 | tf_op jit(solution)/shard_map/reduce_sum | solution.py:193
  214.7 1.1 collective-permute-start.11
  215.9 2.9 %copy.19 = f32[1024,512]{1,0:T(8,128)} copy(f32[1024,512]{0,1:T(8,128)} %get-tuple-element.32) | data formatting | bytes 4194304
  219.4 2.2 collective-permute-start.12
  221.6 1.4 collective-permute-done.12
  223.7 2.2 collective-permute-start.13
  225.9 1.4 collective-permute-done.13
  228.0 2.8 %collective-permute-start.14 = (f32[1]{0:T(128)}, f32[1]{0:T(128)}, u32[]{:S(2)}, u32[]{:S(2)}) collective-permute-start(f32[1]{0:T(128)} %add.143), channel_id=1, source_target_pairs={{0,1},{1,0},{2,3},{3,2},{4,5},{5,4},{6,7},{7,6},{8,9},{9,8},{10,11... | collective-permute-start | bytes 20 | tf_op jit(solution)/shard_map/ppermute | solution.py:32
  232.2 3.3 %collective-permute-start.15 = (f32[1]{0:T(128)}, f32[1]{0:T(128)}, u32[]{:S(2)}, u32[]{:S(2)}) collective-permute-start(f32[1]{0:T(128)} %add.144), channel_id=1, source_target_pairs={{0,2},{1,3},{2,0},{3,1},{4,6},{5,7},{6,4},{7,5},{8,10},{9,11},{10,... | collective-permute-start | bytes 20 | tf_op jit(solution)/shard_map/ppermute | solution.py:32
  235.5 1.2 collective-permute-done.15
  (93 shorter events, 8.8 us)
Async XLA Ops:
  7.2 76.2 %all-gather.8.cloned.1.call-start = ((), (), s32[]{:S(2)}) async-start(), calls=%async_computation | async-start | bytes 2621440 | tf_op jit(solution)/shard_map/all_gather | solution.py:67
  8.5 1.9 copy-start.7
  8.5 1.9 copy-start.9
  8.6 17.6 %copy-start.13 = (f32[64]{0:T(128)S(1)}, f32[64]{0:T(128)}, u32[]{:S(2)}) copy-start(f32[64]{0:T(128)} %param.18) | copy-start | bytes 772
  8.6 17.6 %copy-start.11 = (f32[768]{0:T(1024)S(1)}, f32[768]{0:T(1024)}, u32[]{:S(2)}) copy-start(f32[768]{0:T(1024)} %param.11) | copy-start | bytes 9220
  8.6 18.3 %copy-start.8 = (bf16[768,64]{0,1:T(8,128)(2,1)S(1)}, bf16[768,64]{0,1:T(8,128)(2,1)}, u32[]{:S(2)}) copy-start(bf16[768,64]{0,1:T(8,128)(2,1)} %param.10) | copy-start | bytes 294916
  9.6 113.6 %all-gather.10.cloned.1.call-start = ((), (), s32[]{:S(2)}) async-start(), calls=%async_computation.1 | async-start | bytes 2621440 | tf_op jit(solution)/shard_map/all_gather | solution.py:67
  37.6 10.1 %copy-start.1 = (bf16[3072,67]{0,1:T(8,128)(2,1)}, bf16[3072,67]{0,1:T(8,128)(2,1)S(1)}, u32[]{:S(2)}) copy-start(bf16[3072,67]{0,1:T(8,128)(2,1)S(1)} %all_gather.34) | copy-start | bytes 1234948
  47.2 10.6 %copy-start.14 = (f32[2]{0:T(128)S(1)}, f32[2]{0:T(128)}, u32[]{:S(2)}) copy-start(f32[2]{0:T(128)} %param.19) | copy-start | bytes 28
  59.0 1.0 slice-start.2
  84.8 38.2 %collective-permute-start = (bf16[1,64,4096]{2,1,0:T(8,128)(2,1)S(1)}, bf16[1,64,4096]{2,1,0:T(8,128)(2,1)S(1)}, u32[]{:S(2)}, u32[]{:S(2)}) collective-permute-start(bf16[1,64,4096]{2,1,0:T(8,128)(2,1)S(1)} %get-tuple-element.38), channel_id=1, source_target_pairs={{0,8},{8,0},{16,24},{24,16},{1,9},{9,1},{17,25},{25,17},{2,10},{10... | collective-permute-start | bytes 1572872 | tf_op jit(solution)/shard_map/ppermute | solution.py:123
  85.7 37.3 %collective-permute-start.1 = (bf16[1,64,4096]{2,1,0:T(8,128)(2,1)S(1)}, bf16[1,64,4096]{2,1,0:T(8,128)(2,1)S(1)}, u32[]{:S(2)}, u32[]{:S(2)}) collective-permute-start(bf16[1,64,4096]{2,1,0:T(8,128)(2,1)S(1)} %get-tuple-element.37), channel_id=1, source_target_pairs={{0,16},{8,24},{16,0},{24,8},{1,17},{9,25},{17,1},{25,9},{2,18},{10... | collective-permute-start | bytes 1572872 | tf_op jit(solution)/shard_map/ppermute | solution.py:123
  86.9 36.1 %collective-permute-start.2 = (bf16[1,64,4096]{2,1,0:T(8,128)(2,1)S(1)}, bf16[1,64,4096]{2,1,0:T(8,128)(2,1)S(1)}, u32[]{:S(2)}, u32[]{:S(2)}) collective-permute-start(bf16[1,64,4096]{2,1,0:T(8,128)(2,1)S(1)} %get-tuple-element.36), channel_id=1, source_target_pairs={{0,24},{8,16},{16,8},{24,0},{1,25},{9,17},{17,9},{25,1},{2,26},{10... | collective-permute-start | bytes 1572872 | tf_op jit(solution)/shard_map/ppermute | solution.py:123
  123.2 4.4 %collective-permute-start.3 = (bf16[256,4096]{1,0:T(8,128)(2,1)S(1)}, bf16[256,4096]{1,0:T(8,128)(2,1)}, u32[]{:S(2)}, u32[]{:S(2)}) collective-permute-start(bf16[256,4096]{1,0:T(8,128)(2,1)S(1)} %bitcast.51), channel_id=1, source_target_pairs={{0,4},{4,0},{1,5},{5,1},{2,6},{6,2},{3,7},{7,3},{8,12},{12,8},{9,1... | collective-permute-start | bytes 6291464 | tf_op jit(solution)/shard_map/ppermute | solution.py:135
  123.3 2.3 copy-start.6
  129.7 22.8 %collective-permute-start.4 = (bf16[1,64,4096]{2,1,0:T(8,128)(2,1)S(1)}, bf16[1,64,4096]{2,1,0:T(8,128)(2,1)S(1)}, u32[]{:S(2)}, u32[]{:S(2)}) collective-permute-start(bf16[1,64,4096]{2,1,0:T(8,128)(2,1)S(1)} %get-tuple-element.35), channel_id=1, source_target_pairs={{0,8},{8,0},{16,24},{24,16},{1,9},{9,1},{17,25},{25,17},{2,10},{10... | collective-permute-start | bytes 1572872 | tf_op jit(solution)/shard_map/ppermute | solution.py:123
  130.5 21.9 %collective-permute-start.5 = (bf16[1,64,4096]{2,1,0:T(8,128)(2,1)S(1)}, bf16[1,64,4096]{2,1,0:T(8,128)(2,1)S(1)}, u32[]{:S(2)}, u32[]{:S(2)}) collective-permute-start(bf16[1,64,4096]{2,1,0:T(8,128)(2,1)S(1)} %get-tuple-element.34), channel_id=1, source_target_pairs={{0,16},{8,24},{16,0},{24,8},{1,17},{9,25},{17,1},{25,9},{2,18},{10... | collective-permute-start | bytes 1572872 | tf_op jit(solution)/shard_map/ppermute | solution.py:123
  131.8 24.4 %collective-permute-start.6 = (bf16[1,64,4096]{2,1,0:T(8,128)(2,1)S(1)}, bf16[1,64,4096]{2,1,0:T(8,128)(2,1)S(1)}, u32[]{:S(2)}, u32[]{:S(2)}) collective-permute-start(bf16[1,64,4096]{2,1,0:T(8,128)(2,1)S(1)} %get-tuple-element.33), channel_id=1, source_target_pairs={{0,24},{8,16},{16,8},{24,0},{1,25},{9,17},{17,9},{25,1},{2,26},{10... | collective-permute-start | bytes 1572872 | tf_op jit(solution)/shard_map/ppermute | solution.py:123
  158.6 9.3 %collective-permute-start.8 = (bf16[256,4096]{1,0:T(8,128)(2,1)}, bf16[256,4096]{1,0:T(8,128)(2,1)}, u32[]{:S(2)}, u32[]{:S(2)}) collective-permute-start(bf16[256,4096]{1,0:T(8,128)(2,1)} %bitcast.15), channel_id=1, source_target_pairs={{0,4},{4,0},{1,5},{5,1},{2,6},{6,2},{3,7},{7,3},{8,12},{12,8},{9,1... | collective-permute-start | bytes 6291464 | tf_op jit(solution)/shard_map/ppermute | solution.py:135
  165.1 1.3 copy-start.3
  166.4 22.5 %slice-start = ((s8[6291456]{0:T(1024)(128)(4,1)}), s8[4194304]{0:T(1024)(128)(4,1)S(1)}, s32[]{:S(2)}) async-start(s8[6291456]{0:T(1024)(128)(4,1)} %bitcast.53), calls=%async_computation.2 | async-start | bytes 8388608
  167.4 21.4 %slice-start.1 = ((s8[6291456]{0:T(1024)(128)(4,1)}), s8[2097152]{0:T(1024)(128)(4,1)S(1)}, s32[]{:S(2)}) async-start(s8[6291456]{0:T(1024)(128)(4,1)} %bitcast.53), calls=%async_computation.3 | async-start | bytes 4194304
  167.4 39.7 %collective-permute-start.7 = (f32[1024,256]{0,1:T(8,128)}, f32[1024,256]{0,1:T(8,128)S(1)}, u32[]{:S(2)}, u32[]{:S(2)}) collective-permute-start(f32[1024,256]{0,1:T(8,128)} %slice.66), channel_id=1, source_target_pairs={{0,4},{4,0},{1,5},{5,1},{2,6},{6,2},{3,7},{7,3},{8,12},{12,8},{9,1... | collective-permute-start | bytes 3145736 | tf_op jit(solution)/shard_map/ppermute | solution.py:183
  194.3 2.3 copy-start.4
  194.3 1.3 copy-start.2
  195.4 13.3 %collective-permute-start.9 = (f32[1024,256]{0,1:T(8,128)}, f32[1024,256]{0,1:T(8,128)}, u32[]{:S(2)}, u32[]{:S(2)}) collective-permute-start(f32[1024,256]{0,1:T(8,128)} %slice.68), channel_id=1, source_target_pairs={{0,4},{4,0},{1,5},{5,1},{2,6},{6,2},{3,7},{7,3},{8,12},{12,8},{9,1... | collective-permute-start | bytes 3145736 | tf_op jit(solution)/shard_map/ppermute | solution.py:183
  196.6 7.9 %collective-permute-start.10 = (f32[1024]{0:T(1024)S(1)}, f32[1024]{0:T(1024)S(1)}, u32[]{:S(2)}, u32[]{:S(2)}) collective-permute-start(f32[1024]{0:T(1024)S(1)} %convolution_reduce_fusion), channel_id=1, source_target_pairs={{0,4},{4,0},{1,5},{5,1},{2,6},{6,2},{3,7},{7,3},{8,12},{12,8},{9,1... | collective-permute-start | bytes 12296 | tf_op jit(solution)/shard_map/ppermute | solution.py:185
  198.8 5.6 %copy-start.10 = (f32[1024]{0:T(1024)S(1)}, f32[1024]{0:T(1024)}, u32[]{:S(2)}) copy-start(f32[1024]{0:T(1024)} %param.14) | copy-start | bytes 12292
  198.8 5.6 %copy-start.12 = (f32[1024]{0:T(1024)S(1)}, f32[1024]{0:T(1024)}, u32[]{:S(2)}) copy-start(f32[1024]{0:T(1024)} %param.17) | copy-start | bytes 12292
  207.1 1.9 copy-start.5
  208.6 2.0 copy-start
  214.7 4.0 %collective-permute-start.11 = (f32[1]{0:T(128)}, f32[1]{0:T(128)}, u32[]{:S(2)}, u32[]{:S(2)}) collective-permute-start(f32[1]{0:T(128)} %bitcast.17), channel_id=1, source_target_pairs={{0,4},{4,0},{1,5},{5,1},{2,6},{6,2},{3,7},{7,3},{8,12},{12,8},{9,1... | collective-permute-start | bytes 20 | tf_op jit(solution)/shard_map/ppermute | solution.py:32
  219.4 3.6 %collective-permute-start.12 = (f32[1]{0:T(128)}, f32[1]{0:T(128)}, u32[]{:S(2)}, u32[]{:S(2)}) collective-permute-start(f32[1]{0:T(128)} %add.141), channel_id=1, source_target_pairs={{0,16},{16,0},{1,17},{17,1},{2,18},{18,2},{3,19},{19,3},{4,20},{20... | collective-permute-start | bytes 20 | tf_op jit(solution)/shard_map/ppermute | solution.py:32
  223.7 3.6 %collective-permute-start.13 = (f32[1]{0:T(128)}, f32[1]{0:T(128)}, u32[]{:S(2)}, u32[]{:S(2)}) collective-permute-start(f32[1]{0:T(128)} %add.142), channel_id=1, source_target_pairs={{0,8},{8,0},{1,9},{9,1},{2,10},{10,2},{3,11},{11,3},{4,12},{12,4},... | collective-permute-start | bytes 20 | tf_op jit(solution)/shard_map/ppermute | solution.py:32
  228.0 3.6 %collective-permute-start.14 = (f32[1]{0:T(128)}, f32[1]{0:T(128)}, u32[]{:S(2)}, u32[]{:S(2)}) collective-permute-start(f32[1]{0:T(128)} %add.143), channel_id=1, source_target_pairs={{0,1},{1,0},{2,3},{3,2},{4,5},{5,4},{6,7},{7,6},{8,9},{9,8},{10,11... | collective-permute-start | bytes 20 | tf_op jit(solution)/shard_map/ppermute | solution.py:32
  232.2 4.5 %collective-permute-start.15 = (f32[1]{0:T(128)}, f32[1]{0:T(128)}, u32[]{:S(2)}, u32[]{:S(2)}) collective-permute-start(f32[1]{0:T(128)} %add.144), channel_id=1, source_target_pairs={{0,2},{1,3},{2,0},{3,1},{4,6},{5,7},{6,4},{7,5},{8,10},{9,11},{10,... | collective-permute-start | bytes 20 | tf_op jit(solution)/shard_map/ppermute | solution.py:32
Sparse Core Ops, SparseCore 0:
  9.8 48.7 all-gather.7
  60.1 44.5 all-gather.9
